TPU v7x, 256 devices: a whole 4x4x8 slice. The times are simulated.
256 devices in a mesh: prow: 16 (over z, core), pcol: 16 (over x, y).
Axes of the slice: x: 4, y: 4, z: 8, core: 2. Of those that a mesh axis runs over, the one named last changes fastest.
Arguments:
- inv_lead: float32 [4, 16, 256, 4, 16, 256], P(None, 'prow', None, None, 'pcol'), may hold values from -1 to 2, as said below
- h_lead: float32 [4, 16, 256, 6, 16, 256], P(None, 'pcol', None, None, 'prow'), may hold values from -6 to 6
- h_slab: float32 [512, 6, 16, 256], P('pcol', None, 'prow'), may hold values from -6 to 6
- l_panel: float32 [512, 4, 16, 256], P('pcol', None, 'prow'), may hold values from -0.046875 to 0.046875
- l_diag: float32 [512, 512], replicated, may hold values from -1 to 2, as said below
Outputs:
- x_slab: float32 [512, 6, 16, 256], P('pcol', None, 'prow')
- y_lead: float32 [512, 4, 16, 256], P('pcol', None, 'prow')
- y_diag: float32 [512, 512], P('pcol', 'prow')
Inputs may be any that keep to these rules, and one draw needn't show every extreme that they name: inv_lead is lower triangular in natural order, with diagonal entries between 1 and 2. l_diag is lower triangular, with diagonal entries between 1 and 2.
All inputs are finite; a program needn't handle non-finite values.
Results may differ from a plain program's by a relative error of at most 0.00018.
Values sent between devices are 32-bit elements; how exact they have to be, the bound alone decides.
No kernel may reach another device: no remote copies, remote signals or barrier semaphores. Data moves between devices by JAX's collectives and lax.ppermute only.
A program may use at most 128 MiB of HBM per device.

v0:
```python
import jax
import jax.numpy as jnp
from jax import lax
from jax.sharding import PartitionSpec as P


def copy_for_each(value, axis):
    copies = jnp.broadcast_to(value, (lax.axis_size(axis), *value.shape))
    return lax.all_to_all(copies, axis, split_axis=0, concat_axis=0, tiled=True)


def joined_along(parts, dim):
    lengths = list(parts.shape[1:])
    lengths[dim] *= parts.shape[0]
    return jnp.moveaxis(parts, 0, dim).reshape(lengths)


def gathered_copies(value, axis, dim):
    parts = copy_for_each(value, axis)
    return joined_along(parts, dim)


def in_blocks(value, dim, size):
    lengths = value.shape
    parts = value.reshape(*lengths[:dim], size, lengths[dim] // size, *lengths[dim + 1 :])
    return jnp.moveaxis(parts, dim, 0)


def sum_at_owner(value, axis, dim):
    parts = in_blocks(value, dim, lax.axis_size(axis))
    arrived = lax.all_to_all(parts, axis, split_axis=0, concat_axis=0, tiled=True)
    return arrived.sum(axis=0)


def in_one_piece(arrays, axis, dim, along):
    widths = [a.shape[along] for a in arrays]
    both = jnp.concatenate(arrays, axis=along)
    result = lax.psum_scatter(both, axis, scatter_dimension=dim, tiled=True)
    return tuple(jnp.split(result, [sum(widths[:k]) for k in range(1, len(widths))], axis=along))


def matmul_hi(left, right):
    return jnp.dot(left, right, precision=lax.Precision.HIGHEST, preferred_element_type=jnp.float32)


def matmul_trans(left, right):
    return lax.dot_general(
        left,
        right,
        (((1,), (1,)), ((), ())),
        precision=lax.Precision.HIGHEST,
        preferred_element_type=jnp.float32,
    )


def invert_diag(l_diag, block_size):
    diag_top = l_diag[:block_size, :block_size]
    diag_bottom = l_diag[block_size:, block_size:]
    off_block = l_diag[block_size:, :block_size]
    identity = jnp.eye(block_size, dtype=jnp.float32)
    top_inv = lax.linalg.triangular_solve(diag_top, identity, left_side=True, lower=True)
    bottom_inv = lax.linalg.triangular_solve(diag_bottom, identity, left_side=True, lower=True)
    corner = -matmul_hi(bottom_inv, matmul_hi(off_block, top_inv))
    upper_rows = jnp.concatenate([top_inv, jnp.zeros_like(top_inv)], axis=1)
    lower_rows = jnp.concatenate([corner, bottom_inv], axis=1)
    return jnp.concatenate([upper_rows, lower_rows], axis=0)


def per_device(inv_lead, h_lead, h_slab, l_panel, l_diag):
    slab_rows = l_diag.shape[0]
    block_size = l_panel.shape[3]
    prev_blocks = l_panel.shape[1]
    x_rows = l_panel.shape[0]
    h_blocks = h_slab.shape[1]
    diag_inv = invert_diag(l_diag, slab_rows // 2)
    inv_local = inv_lead.reshape(prev_blocks * block_size, -1)
    col_width = inv_local.shape[1]
    col_blocks = col_width // block_size
    h_local = h_lead.reshape(col_width, -1)
    h_side = h_slab.reshape(x_rows, -1)
    y_rows = slab_rows // lax.axis_size("prow")
    row_start = lax.axis_index("prow") * y_rows
    col_start = lax.axis_index("pcol") * x_rows
    piece = gathered_copies(l_panel, "pcol", 0)
    factor = matmul_hi(diag_inv, piece.reshape(piece.shape[0], -1))
    side_term = matmul_hi(lax.dynamic_slice_in_dim(diag_inv, col_start, x_rows, 1), h_side)
    own_panel = sum_at_owner(-matmul_hi(factor, inv_local), "prow", 0)
    product = matmul_hi(lax.all_gather(own_panel, "prow", axis=0, tiled=True), h_local)
    x_local = sum_at_owner(product + side_term, "pcol", 0)
    x_slab = x_local.reshape(x_rows, h_blocks, 1, block_size)
    kept_cols = x_slab[:, : prev_blocks + 1]
    widened = lax.all_gather(kept_cols, "prow", axis=2, tiled=True).reshape(x_rows, -1)
    prev_rows = prev_blocks * block_size * lax.axis_size("prow")
    head_cols = widened[:, :prev_rows]
    tail_cols = widened[:, prev_rows : prev_rows + slab_rows]
    shifted_x = lax.all_to_all(
        head_cols.reshape(x_rows, col_blocks, lax.axis_size("pcol"), block_size),
        "pcol",
        split_axis=2,
        concat_axis=0,
        tiled=True,
    )
    shifted_x = shifted_x.reshape(slab_rows, col_width)
    lead_part = matmul_trans(shifted_x, inv_local)
    diag_part = matmul_trans(shifted_x, own_panel)
    y_first, y_block = in_one_piece((lead_part, diag_part), "pcol", 0, 1)
    diag_rows = lax.dynamic_slice_in_dim(diag_inv, row_start, y_rows, 0)
    y_diag = y_block + matmul_trans(tail_cols, diag_rows)
    return (x_slab, y_first.reshape(x_rows, prev_blocks, 1, block_size), y_diag)


def solution(mesh):
    return jax.shard_map(
        per_device,
        mesh=mesh,
        in_specs=(
            P(None, "prow", None, None, "pcol", None),
            P(None, "pcol", None, None, "prow", None),
            P("pcol", None, "prow", None),
            P("pcol", None, "prow", None),
            P(),
        ),
        out_specs=(P("pcol", None, "prow", None), P("pcol", None, "prow", None), P("pcol", "prow")),
        check_vma=False,
    )
```

profile of v0, /device:TPU:2, one launch (start us, length us, event | category | flops | bytes accessed | tf_op | source)
XLA Modules:
  0.0 457.1 jit_solution(1383191247335577584)
XLA Ops:
  8.1 2.9 broadcast_in_dim.4
  11.1 7.5 %all-to-all-start = ((f32[16,32,4,1,256]{4,3,2,1,0:T(1,128)}), f32[16,32,4,1,256]{4,3,2,1,0:T(1,128)S(1)}, u32[]{:S(2)}, u32[]{:S(2)}) async-start(f32[16,32,4,1,256]{4,3,2,1,0:T(1,128)} %broadcast_in_dim.4), calls=%async_computation | async-start | bytes 4194304 | tf_op jit(solution)/shard_map/all_to_all | solution.py:9
  19.8 3.8 while.4
  23.6 19.7 %custom-call.4 = f32[2,128,128]{1,2,0:T(8,128)S(1)} custom-call(f32[2,128,128]{2,1,0:T(8,128)S(1)} %get-tuple-element.18), custom_call_target="InvertDiagBlocksLowerTriangular" | custom-call | tf_op jit(solution)/shard_map/triangular_solve/custom-call.1 | solution.py:61
  43.3 4.0 while.5
  43.9 1.4 bitcast_dynamic-update-slice_fusion.5
  45.9 1.4 bitcast_dynamic-update-slice_fusion.5
  47.3 19.7 %custom-call.5 = f32[2,128,128]{1,2,0:T(8,128)S(1)} custom-call(f32[2,128,128]{2,1,0:T(8,128)S(1)} %get-tuple-element.19), custom_call_target="InvertDiagBlocksLowerTriangular" | custom-call | tf_op jit(solution)/shard_map/triangular_solve/custom-call.1 | solution.py:62
  67.0 14.2 %reduce.1 = f32[4,256,4,256]{3,2,1,0:T(4,128)} reduce(f32[4,1,256,4,1,256]{5,4,3,2,1,0:T(1,128)} %param.7, f32[]{:T(128)} %constant.47), dimensions={1,4}, to_apply=%param.7.reduce_sub_computation | reduce | bytes 8388612 | tf_op args[0]
  81.2 5.2 %copy.34 = f32[128,8,4,256]{3,1,2,0:T(8,128)} copy(f32[128,8,4,256]{3,2,1,0:T(4,128)} %bitcast.82) | data formatting | bytes 8388608
  88.2 1.5 fusion.6
  90.2 7.4 %reduce = f32[16,32,4,256]{3,2,1,0:T(4,128)} reduce(f32[16,32,4,1,256]{4,3,2,1,0:T(1,128)S(1)} %all-to-all-done, f32[]{:T(128)} %constant.47), dimensions={3}, to_apply=%all_to_all.20.reduce_sub_computation | reduce | bytes 4194308 | tf_op jit(solution)/shard_map/all_to_all | solution.py:9
  97.6 2.1 copy.33
  99.7 4.0 fusion.22
  103.7 6.9 %convolution_negate_fusion = f32[512,1024]{1,0:T(8,128)S(1)} fusion(f32[512,1024]{1,0:T(8,128)S(1)} %fusion.22, f32[1024,1024]{1,0:T(8,128)S(1)} %bitcast.77), kind=kOutput, calls=%fused_computation.6 | convolution fusion | flops 6442975232 | bytes 8388608 | tf_op jit(solution)/shard_map/dot_general | solution.py:43
  110.6 58.0 %all_to_all.31 = f32[16,32,1024]{2,1,0:T(8,128)S(1)} all-to-all(f32[16,32,1024]{2,1,0:T(8,128)S(1)} %bitcast.92), channel_id=1, replica_groups=mesh['prow'=16,'pcol'=16] {'prow'}, dimensions={0} | all-to-all | bytes 4194304 | tf_op jit(solution)/shard_map/all_to_all | solution.py:31
  169.5 37.4 %reduce.2 = f32[4,256,6,256]{3,2,1,0:T(8,128)} reduce(f32[4,1,256,6,1,256]{5,4,3,2,1,0:T(1,128)} %param.8, f32[]{:T(128)} %constant.47), dimensions={1,4}, to_apply=%param.8.reduce_sub_computation | reduce | bytes 12582916 | tf_op args[1]
  206.8 9.2 %copy.35 = f32[128,8,6,256]{3,1,2,0:T(8,128)} copy(f32[128,8,6,256]{3,2,1,0:T(8,128)} %bitcast.79) | data formatting | bytes 12582912
  216.8 13.7 %fusion.25 = f32[512,1536]{1,0:T(8,128)S(1)} fusion(f32[512,1024]{1,0:T(8,128)} %all-gather.3.cloned.1.call-done, f32[1024,1536]{1,0:T(8,128)} %bitcast.93), kind=kOutput, calls=%fused_computation.47 | convolution fusion | flops 9663676416 | bytes 11534336 | tf_op jit(solution)/shard_map/dot_general | solution.py:43
  230.4 2.8 convolution_add_fusion
  233.2 45.1 %all_to_all.32 = f32[16,32,1536]{2,1,0:T(8,128)S(1)} all-to-all(f32[16,32,1536]{2,1,0:T(8,128)S(1)} %bitcast.83), channel_id=1, replica_groups=mesh['prow'=16,'pcol'=16] {'pcol'}, dimensions={0} | all-to-all | bytes 6291456 | tf_op jit(solution)/shard_map/all_to_all | solution.py:31
  279.4 36.6 %all-gather.5.cloned.1.call-done = f32[32,5,16,256]{3,0,1,2:T(8,128)} async-done(((f32[32,5,1,256]{3,0,1,2:T(8,128)}), f32[32,5,16,256]{3,0,1,2:T(8,128)}) %all-gather.5.cloned.1.call-update) | async-done | bytes 2621456 | tf_op jit(solution)/shard_map/all_gather | solution.py:92
  315.9 3.3 copy.25
  319.2 1.5 copy.37
  321.5 1.4 copy.26
  322.9 33.8 %all_to_all.30 = f32[32,4,16,256]{3,1,0,2:T(4,128)S(1)} all-to-all(f32[32,4,16,256]{3,1,0,2:T(4,128)S(1)} %copy.26), channel_id=1, replica_groups=mesh['prow'=16,'pcol'=16] {'pcol'}, dimensions={2} | all-to-all | bytes 4194304 | tf_op jit(solution)/shard_map/all_to_all | solution.py:96
  357.1 1.7 copy-done.1
  358.8 7.0 %fusion.26 = f32[512,1024]{1,0:T(8,128)S(1)} fusion(f32[512,1024]{1,0:T(8,128)S(1)} %bitcast.80, f32[1024,1024]{1,0:T(8,128)S(1)} %bitcast.78), kind=kOutput, calls=%fused_computation.48 | convolution fusion | flops 6442450944 | bytes 8388608 | tf_op jit(solution)/shard_map/dot_general | solution.py:47
  365.8 1.8 fusion.27
  367.6 1.6 pad_maximum_fusion
  370.1 76.6 %reduce-scatter.2.cloned.1.call-done = f32[32,1056]{1,0:T(8,128)} async-done(((f32[512,1056]{1,0:T(8,128)}), f32[32,1056]{1,0:T(8,128)}) %reduce-scatter.2.cloned.1.call-update) | async-done | bytes 135184 | tf_op jit(solution)/shard_map/reduce_scatter | solution.py:38
  448.5 1.6 convolution_add_fusion.1
  (55 shorter events, 15.7 us)
Async XLA Ops:
  11.1 79.2 %all-to-all-start = ((f32[16,32,4,1,256]{4,3,2,1,0:T(1,128)}), f32[16,32,4,1,256]{4,3,2,1,0:T(1,128)S(1)}, u32[]{:S(2)}, u32[]{:S(2)}) async-start(f32[16,32,4,1,256]{4,3,2,1,0:T(1,128)} %broadcast_in_dim.4), calls=%async_computation | async-start | bytes 4194304 | tf_op jit(solution)/shard_map/all_to_all | solution.py:9
  18.5 198.2 %all-gather.3.cloned.1.call-start = ((), (), s32[]{:S(2)}) async-start(), calls=%async_computation.5 | async-start | bytes 2228224 | tf_op jit(solution)/shard_map/all_gather | solution.py:88
  99.7 4.0 copy-start
  169.4 146.5 %all-gather.5.cloned.1.call-start = ((), (), s32[]{:S(2)}) async-start(), calls=%async_computation.6 | async-start | bytes 2785280 | tf_op jit(solution)/shard_map/all_gather | solution.py:92
  206.8 9.2 %copy-start.4 = (f32[32,6,1,256]{3,2,1,0:T(1,128)S(1)}, f32[32,6,1,256]{3,2,1,0:T(1,128)}, u32[]{:S(2)}) copy-start(f32[32,6,1,256]{3,2,1,0:T(1,128)} %param.9) | copy-start | bytes 589828
  216.7 13.7 %copy-start.2 = (f32[512,512]{1,0:T(8,128)}, f32[512,512]{1,0:T(8,128)S(1)}, u32[]{:S(2)}) copy-start(f32[512,512]{1,0:T(8,128)S(1)} %select_maximum_fusion) | copy-start | bytes 3145732
  279.3 167.4 %reduce-scatter.2.cloned.1.call-start = ((), (), s32[]{:S(2)}) async-start(), calls=%async_computation.7 | async-start | bytes 2506752 | tf_op jit(solution)/shard_map/reduce_scatter | solution.py:38
  356.7 2.2 copy-start.1
  358.8 7.0 %copy-start.3 = (f32[32,1024]{1,0:T(8,128)S(1)}, f32[32,1024]{1,0:T(8,128)}, u32[]{:S(2)}) copy-start(f32[32,1024]{1,0:T(8,128)} %reduce_sum.18) | copy-start | bytes 393220
Sparse Core Ops, SparseCore 0:
  169.5 37.7 all-gather.2
  279.4 36.4 all-gather.4
  369.4 77.3 reduce-scatter.1
where the time goes:
time: 464 us; the launch traced here: 457 us
  blocking collectives  137 us (30%)
  waiting for transfers between devices  113 us (24%)
  other arithmetic  103 us (22%)
  matrix products  41.4 us (9%)
  local copies, waits for them, and re-layouts  40.7 us (9%)
  between operations  14.5 us (3%)
  starting transfers between devices  7.6 us (2%)
    all_to_all x2, blocking collectives, sum_at_owner(): lax.all_to_all(parts, axis, split_axis=0, concat_axis=0, tiled=True)  103 us
    reduce_scatter x1, waiting for transfers between devices, in_one_piece(): result = lax.psum_scatter(both, axis, scatter_dimension=dim, tiled=True)  76.6 us
    unnamed x3, other arithmetic  52.1 us
    all_gather x1, waiting for transfers between devices, per_device(): lax.all_gather(kept_cols, 'prow', axis=2, tiled=True).reshape(x_rows, -1)  36.6 us
    all_to_all x1, blocking collectives, per_device(): lax.all_to_all(head_cols.reshape(x_rows, col_blocks, lax.axis_size('pcol'...  33.8 us
    dot_general x6, matrix products, matmul_hi(): jnp.dot(left, right, precision=lax.Precision.HIGHEST, preferred_element_t...  29.3 us
    unnamed x19, local copies, waits for them, and re-layouts  22.7 us
    another operation x2, other arithmetic, invert_diag(): lax.linalg.triangular_solve(diag_bottom, identity, left_side=True, lower=...  20.7 us
  transfers between devices with their start and end apart: 4, of which 2 were waited for; matrix products, arithmetic and copies ran while one was open for 26% of the time, Pallas kernels for 0%

commit v1 on v0

--- a/solution.py
+++ b/solution.py
@@ -2,6 +2,11 @@
 import jax.numpy as jnp
 from jax import lax
 from jax.sharding import PartitionSpec as P
+
+
+def exchange_gather(block, name, dim):
+    sent = jnp.stack([block] * lax.axis_size(name))
+    return jnp.concatenate(lax.all_to_all(sent, name, 0, 0), axis=dim)
 
 
 def copy_for_each(value, axis):
@@ -89,7 +94,7 @@
     x_local = sum_at_owner(product + side_term, "pcol", 0)
     x_slab = x_local.reshape(x_rows, h_blocks, 1, block_size)
     kept_cols = x_slab[:, : prev_blocks + 1]
-    widened = lax.all_gather(kept_cols, "prow", axis=2, tiled=True).reshape(x_rows, -1)
+    widened = exchange_gather(kept_cols, "prow", 2).reshape(x_rows, -1)
     prev_rows = prev_blocks * block_size * lax.axis_size("prow")
     head_cols = widened[:, :prev_rows]
     tail_cols = widened[:, prev_rows : prev_rows + slab_rows]

time: 464 us -> 490 us (1.056)
  blocking collectives: 137 us -> 200 us
  waiting for transfers between devices: 113 us -> 76.1 us
    all_to_all x0 -> x1, blocking collectives: none -> 64.4 us  [exchange_gather(): return jnp.concatenate(lax.all_to_all(sent, name, 0, 0), axis=dim)]
    all_gather x1 -> x0, waiting for transfers between devices: 36.6 us -> none  [per_device(): lax.all_gather(kept_cols, 'prow', axis=2, tiled=True).reshape(x_rows, -1)]
    unnamed x19 -> x20, local copies, waits for them, and re-layouts: 22.7 us -> 21.2 us
  transfers between devices with their start and end apart: 4 -> 3, of which waited for: 2 -> 1; matrix products, arithmetic and copies ran while one was open for 26% -> 25% of each run, Pallas kernels for 0% -> 0%
where the time goes in v1:
time: 490 us; the launch traced here: 483 us
  blocking collectives  200 us (41%)
  other arithmetic  103 us (21%)
  waiting for transfers between devices  76.1 us (16%)
  matrix products  41.4 us (8%)
  local copies, waits for them, and re-layouts  40.3 us (8%)
  between operations  14.8 us (3%)
  starting transfers between devices  7.56 us (2%)
    all_to_all x2, blocking collectives, sum_at_owner(): lax.all_to_all(parts, axis, split_axis=0, concat_axis=0, tiled=True)  103 us
    reduce_scatter x1, waiting for transfers between devices, in_one_piece(): result = lax.psum_scatter(both, axis, scatter_dimension=dim, tiled=True)  76.1 us
    all_to_all x1, blocking collectives, exchange_gather(): return jnp.concatenate(lax.all_to_all(sent, name, 0, 0), axis=dim)  64.4 us
    unnamed x3, other arithmetic  52.1 us
    all_to_all x1, blocking collectives, per_device(): lax.all_to_all(head_cols.reshape(x_rows, col_blocks, lax.axis_size('pcol'...  32.6 us
    dot_general x6, matrix products, matmul_hi(): jnp.dot(left, right, precision=lax.Precision.HIGHEST, preferred_element_t...  29.3 us
    unnamed x20, local copies, waits for them, and re-layouts  21.2 us
    another operation x2, other arithmetic, invert_diag(): lax.linalg.triangular_solve(diag_bottom, identity, left_side=True, lower=...  20.7 us
  transfers between devices with their start and end apart: 3, of which 1 were waited for; matrix products, arithmetic and copies ran while one was open for 25% of the time, Pallas kernels for 0%

profile of v1, /device:TPU:2, one launch (start us, length us, event | category | flops | bytes accessed | tf_op | source)
XLA Modules:
  0.0 483.0 jit_solution(12511943435566105362)
XLA Ops:
  8.1 2.9 broadcast_in_dim.4
  11.1 7.5 %all-to-all-start = ((f32[16,32,4,1,256]{4,3,2,1,0:T(1,128)}), f32[16,32,4,1,256]{4,3,2,1,0:T(1,128)S(1)}, u32[]{:S(2)}, u32[]{:S(2)}) async-start(f32[16,32,4,1,256]{4,3,2,1,0:T(1,128)} %broadcast_in_dim.4), calls=%async_computation | async-start | bytes 4194304 | tf_op jit(solution)/shard_map/all_to_all | solution.py:14
  19.8 3.8 while.4
  23.6 19.7 %custom-call.4 = f32[2,128,128]{1,2,0:T(8,128)S(1)} custom-call(f32[2,128,128]{2,1,0:T(8,128)S(1)} %get-tuple-element.18), custom_call_target="InvertDiagBlocksLowerTriangular" | custom-call | tf_op jit(solution)/shard_map/triangular_solve/custom-call.1 | solution.py:66
  43.3 4.0 while.5
  43.9 1.4 bitcast_dynamic-update-slice_fusion.5
  45.9 1.4 bitcast_dynamic-update-slice_fusion.5
  47.3 19.7 %custom-call.5 = f32[2,128,128]{1,2,0:T(8,128)S(1)} custom-call(f32[2,128,128]{2,1,0:T(8,128)S(1)} %get-tuple-element.19), custom_call_target="InvertDiagBlocksLowerTriangular" | custom-call | tf_op jit(solution)/shard_map/triangular_solve/custom-call.1 | solution.py:67
  67.0 14.2 %reduce.1 = f32[4,256,4,256]{3,2,1,0:T(4,128)} reduce(f32[4,1,256,4,1,256]{5,4,3,2,1,0:T(1,128)} %param.7, f32[]{:T(128)} %constant.47), dimensions={1,4}, to_apply=%param.7.reduce_sub_computation | reduce | bytes 8388612 | tf_op args[0]
  81.2 5.2 %copy.43 = f32[128,8,4,256]{3,1,2,0:T(8,128)} copy(f32[128,8,4,256]{3,2,1,0:T(4,128)} %bitcast.87) | data formatting | bytes 8388608
  88.2 1.5 fusion.6
  90.2 7.4 %reduce = f32[16,32,4,256]{3,2,1,0:T(4,128)} reduce(f32[16,32,4,1,256]{4,3,2,1,0:T(1,128)S(1)} %all-to-all-done, f32[]{:T(128)} %constant.47), dimensions={3}, to_apply=%all_to_all.23.reduce_sub_computation | reduce | bytes 4194308 | tf_op jit(solution)/shard_map/all_to_all | solution.py:14
  97.6 2.1 copy.42
  99.7 4.0 fusion.22
  103.7 6.9 %convolution_negate_fusion = f32[512,1024]{1,0:T(8,128)S(1)} fusion(f32[512,1024]{1,0:T(8,128)S(1)} %fusion.22, f32[1024,1024]{1,0:T(8,128)S(1)} %bitcast.82), kind=kOutput, calls=%fused_computation.6 | convolution fusion | flops 6442975232 | bytes 8388608 | tf_op jit(solution)/shard_map/dot_general | solution.py:48
  110.6 58.0 %all_to_all.37 = f32[16,32,1024]{2,1,0:T(8,128)S(1)} all-to-all(f32[16,32,1024]{2,1,0:T(8,128)S(1)} %bitcast.95), channel_id=1, replica_groups=mesh['prow'=16,'pcol'=16] {'prow'}, dimensions={0} | all-to-all | bytes 4194304 | tf_op jit(solution)/shard_map/all_to_all | solution.py:36
  169.5 37.4 %reduce.2 = f32[4,256,6,256]{3,2,1,0:T(8,128)} reduce(f32[4,1,256,6,1,256]{5,4,3,2,1,0:T(1,128)} %param.8, f32[]{:T(128)} %constant.47), dimensions={1,4}, to_apply=%param.8.reduce_sub_computation | reduce | bytes 12582916 | tf_op args[1]
  206.8 9.2 %copy.44 = f32[128,8,6,256]{3,1,2,0:T(8,128)} copy(f32[128,8,6,256]{3,2,1,0:T(8,128)} %bitcast.84) | data formatting | bytes 12582912
  216.8 13.7 %fusion.25 = f32[512,1536]{1,0:T(8,128)S(1)} fusion(f32[512,1024]{1,0:T(8,128)} %all-gather.2.cloned.1.call-done, f32[1024,1536]{1,0:T(8,128)} %bitcast.96), kind=kOutput, calls=%fused_computation.48 | convolution fusion | flops 9663676416 | bytes 11534336 | tf_op jit(solution)/shard_map/dot_general | solution.py:48
  230.4 2.8 convolution_add_fusion
  233.2 45.1 %all_to_all.38 = f32[16,32,1536]{2,1,0:T(8,128)S(1)} all-to-all(f32[16,32,1536]{2,1,0:T(8,128)S(1)} %bitcast.88), channel_id=1, replica_groups=mesh['prow'=16,'pcol'=16] {'pcol'}, dimensions={0} | all-to-all | bytes 6291456 | tf_op jit(solution)/shard_map/all_to_all | solution.py:36
  278.9 64.4 %all_to_all.35 = f32[16,32,5,1,256]{4,1,3,2,0:T(8,128)S(1)} all-to-all(f32[16,32,5,1,256]{4,1,3,2,0:T(8,128)S(1)} %stack.2), channel_id=1, replica_groups=mesh['prow'=16,'pcol'=16] {'prow'}, dimensions={0} | all-to-all | bytes 5242880 | tf_op jit(solution)/shard_map/all_to_all | solution.py:9
  343.4 1.5 copy.34
  344.9 1.8 reshape_reshape.7
  346.7 1.6 slice-done
  350.3 32.6 %all_to_all.36 = f32[32,4,16,256]{3,1,0,2:T(4,128)S(1)} all-to-all(f32[32,4,16,256]{3,1,0,2:T(4,128)S(1)} %copy.35), channel_id=1, replica_groups=mesh['prow'=16,'pcol'=16] {'pcol'}, dimensions={2} | all-to-all | bytes 4194304 | tf_op jit(solution)/shard_map/all_to_all | solution.py:101
  383.3 1.7 copy-done.1
  385.1 7.0 %fusion.26 = f32[512,1024]{1,0:T(8,128)S(1)} fusion(f32[512,1024]{1,0:T(8,128)S(1)} %bitcast.85, f32[1024,1024]{1,0:T(8,128)S(1)} %bitcast.83), kind=kOutput, calls=%fused_computation.49 | convolution fusion | flops 6442450944 | bytes 8388608 | tf_op jit(solution)/shard_map/dot_general | solution.py:52
  392.0 1.8 fusion.27
  393.8 1.6 pad_maximum_fusion
  396.3 76.1 %reduce-scatter.2.cloned.1.call-done = f32[32,1056]{1,0:T(8,128)} async-done(((f32[512,1056]{1,0:T(8,128)}), f32[32,1056]{1,0:T(8,128)}) %reduce-scatter.2.cloned.1.call-update) | async-done | bytes 135184 | tf_op jit(solution)/shard_map/reduce_scatter | solution.py:43
  474.1 1.6 convolution_add_fusion.1
  (57 shorter events, 16.5 us)
Async XLA Ops:
  11.1 79.2 %all-to-all-start = ((f32[16,32,4,1,256]{4,3,2,1,0:T(1,128)}), f32[16,32,4,1,256]{4,3,2,1,0:T(1,128)S(1)}, u32[]{:S(2)}, u32[]{:S(2)}) async-start(f32[16,32,4,1,256]{4,3,2,1,0:T(1,128)} %broadcast_in_dim.4), calls=%async_computation | async-start | bytes 4194304 | tf_op jit(solution)/shard_map/all_to_all | solution.py:14
  18.5 198.2 %all-gather.2.cloned.1.call-start = ((), (), s32[]{:S(2)}) async-start(), calls=%async_computation.6 | async-start | bytes 2228224 | tf_op jit(solution)/shard_map/all_gather | solution.py:93
  99.7 4.0 copy-start
  169.4 303.0 %reduce-scatter.2.cloned.1.call-start = ((), (), s32[]{:S(2)}) async-start(), calls=%async_computation.7 | async-start | bytes 2506752 | tf_op jit(solution)/shard_map/reduce_scatter | solution.py:43
  206.8 9.2 %copy-start.5 = (f32[32,6,1,256]{3,2,1,0:T(1,128)S(1)}, f32[32,6,1,256]{3,2,1,0:T(1,128)}, u32[]{:S(2)}) copy-start(f32[32,6,1,256]{3,2,1,0:T(1,128)} %param.9) | copy-start | bytes 589828
  216.7 13.7 %copy-start.3 = (f32[512,512]{1,0:T(8,128)}, f32[512,512]{1,0:T(8,128)S(1)}, u32[]{:S(2)}) copy-start(f32[512,512]{1,0:T(8,128)S(1)} %select_maximum_fusion) | copy-start | bytes 3145732
  346.7 1.6 slice-start
  382.9 2.2 copy-start.1
  385.1 7.0 %copy-start.4 = (f32[32,1024]{1,0:T(8,128)S(1)}, f32[32,1024]{1,0:T(8,128)}, u32[]{:S(2)}) copy-start(f32[32,1024]{1,0:T(8,128)} %reduce_sum.18) | copy-start | bytes 393220
  395.4 78.7 %copy-start.2 = (f32[32,20480]{1,0:T(8,128)S(1)}, f32[32,20480]{1,0:T(8,128)}, u32[]{:S(2)}) copy-start(f32[32,20480]{1,0:T(8,128)} %reshape_reshape.7) | copy-start | bytes 7864324
Sparse Core Ops, SparseCore 0:
  169.5 37.7 all-gather.1
  395.6 76.7 reduce-scatter.1
